TPU v7x, 32 devices: a whole 2x2x4 slice. The times are simulated.
32 devices in a mesh: grp: 8 (over y, x, core), shard: 4 (over z).
Axes of the slice: x: 2, y: 2, z: 4, core: 2. Of those that a mesh axis runs over, the one named last changes fastest.
Arguments:
- hidden_states: bfloat16 [16384, 1024], P(('grp', 'shard')), may hold values from -6 to 6
- output_cotangent: bfloat16 [16384, 1024], P(('grp', 'shard')), may hold values from -6 to 6
- first_gain: float32 [1024], P('shard'), may hold values from 0.5 to 1.5
- first_bias: float32 [1024], P('shard'), may hold values from -0.1875 to 0.1875
- second_gain: float32 [1024], P('shard'), may hold values from 0.5 to 1.5
- second_bias: float32 [1024], P('shard'), may hold values from -0.1875 to 0.1875
- triple_weight: float32 [1024, 3072], P('shard'), may hold values from -0.1875 to 0.1875
- triple_bias: float32 [3072], P('shard'), may hold values from -0.1875 to 0.1875
- output_weight: float32 [1024, 1024], P('shard'), may hold values from -0.5 to 0.5
- output_bias: float32 [1024], P('shard'), may hold values from -0.1875 to 0.1875
- expand_weight: float32 [1024, 4096], P('shard'), may hold values from -0.1875 to 0.1875
- expand_bias: float32 [4096], P('shard'), may hold values from -0.1875 to 0.1875
- shrink_weight: float32 [4096, 1024], P('shard'), may hold values from -0.09375 to 0.09375
- shrink_bias: float32 [1024], P('shard'), may hold values from -0.1875 to 0.1875
- first_gain_momentum: float32 [1024], P('shard'), may hold values from -6 to 6
- first_bias_momentum: float32 [1024], P('shard'), may hold values from -6 to 6
- second_gain_momentum: float32 [1024], P('shard'), may hold values from -6 to 6
- second_bias_momentum: float32 [1024], P('shard'), may hold values from -6 to 6
- triple_weight_momentum: float32 [1024, 3072], P('shard'), may hold values from -6 to 6
- triple_bias_momentum: float32 [3072], P('shard'), may hold values from -6 to 6
- output_weight_momentum: float32 [1024, 1024], P('shard'), may hold values from -6 to 6
- output_bias_momentum: float32 [1024], P('shard'), may hold values from -6 to 6
- expand_weight_momentum: float32 [1024, 4096], P('shard'), may hold values from -6 to 6
- expand_bias_momentum: float32 [4096], P('shard'), may hold values from -6 to 6
- shrink_weight_momentum: float32 [4096, 1024], P('shard'), may hold values from -6 to 6
- shrink_bias_momentum: float32 [1024], P('shard'), may hold values from -6 to 6
- first_gain_variance: float32 [1024], P('shard'), may hold values from 163.84 to 3276.8
- first_bias_variance: float32 [1024], P('shard'), may hold values from 1 to 10
- second_gain_variance: float32 [1024], P('shard'), may hold values from 163.84 to 3276.8
- second_bias_variance: float32 [1024], P('shard'), may hold values from 1 to 10
- triple_weight_variance: float32 [1024, 3072], P('shard'), may hold values from 1 to 10
- triple_bias_variance: float32 [3072], P('shard'), may hold values from 1 to 10
- output_weight_variance: float32 [1024, 1024], P('shard'), may hold values from 1 to 10
- output_bias_variance: float32 [1024], P('shard'), may hold values from 1 to 10
- expand_weight_variance: float32 [1024, 4096], P('shard'), may hold values from 1 to 10
- expand_bias_variance: float32 [4096], P('shard'), may hold values from 1 to 10
- shrink_weight_variance: float32 [4096, 1024], P('shard'), may hold values from 1 to 10
- shrink_bias_variance: float32 [1024], P('shard'), may hold values from 1 to 10
Outputs:
- block_output: bfloat16 [16384, 1024], P(('grp', 'shard'))
- input_gradient: bfloat16 [16384, 1024], P(('grp', 'shard'))
- first_gain_gradient: float32 [1024], P('shard')
- first_bias_gradient: float32 [1024], P('shard')
- second_gain_gradient: float32 [1024], P('shard')
- second_bias_gradient: float32 [1024], P('shard')
- triple_weight_gradient: float32 [1024, 3072], P('shard')
- triple_bias_gradient: float32 [3072], P('shard')
- output_weight_gradient: float32 [1024, 1024], P('shard')
- output_bias_gradient: float32 [1024], P('shard')
- expand_weight_gradient: float32 [1024, 4096], P('shard')
- expand_bias_gradient: float32 [4096], P('shard')
- shrink_weight_gradient: float32 [4096, 1024], P('shard')
- shrink_bias_gradient: float32 [1024], P('shard')
- first_gain_change: float32 [1024], P('shard')
- first_bias_updated: float32 [1024], P('shard')
- second_gain_change: float32 [1024], P('shard')
- second_bias_updated: float32 [1024], P('shard')
- triple_weight_updated: float32 [1024, 3072], P('shard')
- triple_bias_updated: float32 [3072], P('shard')
- output_weight_updated: float32 [1024, 1024], P('shard')
- output_bias_updated: float32 [1024], P('shard')
- expand_weight_updated: float32 [1024, 4096], P('shard')
- expand_bias_updated: float32 [4096], P('shard')
- shrink_weight_updated: float32 [4096, 1024], P('shard')
- shrink_bias_updated: float32 [1024], P('shard')
- first_gain_momentum_updated: float32 [1024], P('shard')
- first_bias_momentum_updated: float32 [1024], P('shard')
- second_gain_momentum_updated: float32 [1024], P('shard')
- second_bias_momentum_updated: float32 [1024], P('shard')
- triple_weight_momentum_updated: float32 [1024, 3072], P('shard')
- triple_bias_momentum_updated: float32 [3072], P('shard')
- output_weight_momentum_updated: float32 [1024, 1024], P('shard')
- output_bias_momentum_updated: float32 [1024], P('shard')
- expand_weight_momentum_updated: float32 [1024, 4096], P('shard')
- expand_bias_momentum_updated: float32 [4096], P('shard')
- shrink_weight_momentum_updated: float32 [4096, 1024], P('shard')
- shrink_bias_momentum_updated: float32 [1024], P('shard')
- first_gain_variance_updated: float32 [1024], P('shard')
- first_bias_variance_updated: float32 [1024], P('shard')
- second_gain_variance_updated: float32 [1024], P('shard')
- second_bias_variance_updated: float32 [1024], P('shard')
- triple_weight_variance_updated: float32 [1024, 3072], P('shard')
- triple_bias_variance_updated: float32 [3072], P('shard')
- output_weight_variance_updated: float32 [1024, 1024], P('shard')
- output_bias_variance_updated: float32 [1024], P('shard')
- expand_weight_variance_updated: float32 [1024, 4096], P('shard')
- expand_bias_variance_updated: float32 [4096], P('shard')
- shrink_weight_variance_updated: float32 [4096, 1024], P('shard')
- shrink_bias_variance_updated: float32 [1024], P('shard')
All inputs are finite; a program needn't handle non-finite values.
Results may differ from a plain program's by a relative error of at most 0.006.
The roundings to bfloat16 on the way count: a program that leaves them out, or rounds other values in their place, can miss the bound.
Values may be sent and summed in bfloat16 or wider, within the bound.
A program may use at most 320 MiB of HBM per device.

v0:
```python
import math

import jax
import jax.numpy as jnp
from jax import lax
from jax.sharding import PartitionSpec as P

HEAD_DIM = 64
ROTARY = 16
STEP = 10


eps_norm = 1e-05
rope_base = 10000.0
beta_one = 0.9
beta_two = 0.95
learn_rate = 0.01
adam_eps = 1e-08
weight_decay = 0.01


def normalize(entries, gain_vec, shift_vec):
    centered = entries - jnp.mean(entries, -1, keepdims=True)
    variance_row = jnp.mean(centered * centered, -1, keepdims=True)
    return centered * lax.rsqrt(variance_row + eps_norm) * gain_vec + shift_vec


def rotary_tables(seq_length):
    position = jnp.arange(seq_length).astype(jnp.float32)[:, None]
    half_rotary = ROTARY // 2
    inverse_freq = rope_base ** (-(jnp.arange(half_rotary).astype(jnp.float32) * 2.0 / ROTARY))
    angles = position * inverse_freq[None, :]
    return (jnp.cos(angles), jnp.sin(angles))


def rotate(tensor, cosine_table, sine_table):
    half_rotary = ROTARY // 2
    first_part = tensor[..., :half_rotary]
    second = tensor[..., half_rotary:ROTARY]
    remain = tensor[..., ROTARY:]
    cos_rows = cosine_table[:, None, :]
    sin_rows = sine_table[:, None, :]
    return jnp.concatenate(
        [
            first_part * cos_rows - second * sin_rows,
            second * cos_rows + first_part * sin_rows,
            remain,
        ],
        -1,
    )


def unrotate(tensor, cosine_table, sine_table):
    half_rotary = ROTARY // 2
    first_part = tensor[..., :half_rotary]
    second = tensor[..., half_rotary:ROTARY]
    remain = tensor[..., ROTARY:]
    cos_rows = cosine_table[:, None, :]
    sin_rows = sine_table[:, None, :]
    return jnp.concatenate(
        [
            first_part * cos_rows + second * sin_rows,
            second * cos_rows - first_part * sin_rows,
            remain,
        ],
        -1,
    )


def to_half(entries):
    return entries.astype(jnp.bfloat16)


def adam_step(weight, gradient, momentum, variance, decayed):
    momentum_new = beta_one * momentum + (1.0 - beta_one) * gradient
    variance_new = beta_two * variance + (1.0 - beta_two) * gradient * gradient
    mean_hat = momentum_new / (1.0 - beta_one**STEP)
    var_hat = variance_new / (1.0 - beta_two**STEP)
    change = mean_hat / (jnp.sqrt(var_hat) + adam_eps)
    if decayed:
        change = change + weight_decay * weight
    delta = -learn_rate * change
    return (weight + delta, delta, momentum_new, variance_new)


def on_device(
    hidden_states,
    output_cotangent,
    first_gain,
    first_bias,
    second_gain,
    second_bias,
    triple_weight,
    triple_bias,
    output_weight,
    output_bias,
    expand_weight,
    expand_bias,
    shrink_weight,
    shrink_bias,
    first_gain_momentum,
    first_bias_momentum,
    second_gain_momentum,
    second_bias_momentum,
    triple_weight_momentum,
    triple_bias_momentum,
    output_weight_momentum,
    output_bias_momentum,
    expand_weight_momentum,
    expand_bias_momentum,
    shrink_weight_momentum,
    shrink_bias_momentum,
    first_gain_variance,
    first_bias_variance,
    second_gain_variance,
    second_bias_variance,
    triple_weight_variance,
    triple_bias_variance,
    output_weight_variance,
    output_bias_variance,
    expand_weight_variance,
    expand_bias_variance,
    shrink_weight_variance,
    shrink_bias_variance,
):
    masters = (
        first_gain,
        first_bias,
        second_gain,
        second_bias,
        triple_weight,
        triple_bias,
        output_weight,
        output_bias,
        expand_weight,
        expand_bias,
        shrink_weight,
        shrink_bias,
    )
    momenta = (
        first_gain_momentum,
        first_bias_momentum,
        second_gain_momentum,
        second_bias_momentum,
        triple_weight_momentum,
        triple_bias_momentum,
        output_weight_momentum,
        output_bias_momentum,
        expand_weight_momentum,
        expand_bias_momentum,
        shrink_weight_momentum,
        shrink_bias_momentum,
    )
    variances = (
        first_gain_variance,
        first_bias_variance,
        second_gain_variance,
        second_bias_variance,
        triple_weight_variance,
        triple_bias_variance,
        output_weight_variance,
        output_bias_variance,
        expand_weight_variance,
        expand_bias_variance,
        shrink_weight_variance,
        shrink_bias_variance,
    )
    gathered = (
        lax.all_gather(to_half(first_gain), "shard", axis=0, tiled=True),
        lax.all_gather(to_half(first_bias), "shard", axis=0, tiled=True),
        lax.all_gather(to_half(second_gain), "shard", axis=0, tiled=True),
        lax.all_gather(to_half(second_bias), "shard", axis=0, tiled=True),
        lax.all_gather(to_half(triple_weight), "shard", axis=0, tiled=True),
        lax.all_gather(to_half(triple_bias), "shard", axis=0, tiled=True),
        lax.all_gather(to_half(output_weight), "shard", axis=0, tiled=True),
        lax.all_gather(to_half(output_bias), "shard", axis=0, tiled=True),
        lax.all_gather(to_half(expand_weight), "shard", axis=0, tiled=True),
        lax.all_gather(to_half(expand_bias), "shard", axis=0, tiled=True),
        lax.all_gather(to_half(shrink_weight), "shard", axis=0, tiled=True),
        lax.all_gather(to_half(shrink_bias), "shard", axis=0, tiled=True),
    )
    (
        gain_one_full,
        bias_one_full,
        gain_two_full,
        bias_two_full,
        triple_full,
        triple_bias_full,
        output_full,
        output_bias_full,
        expand_full,
        expand_bias_full,
        shrink_full,
        shrink_bias_full,
    ) = gathered
    inputs = hidden_states.astype(jnp.float32)
    seq_length, model_width = inputs.shape
    head_count = model_width // HEAD_DIM
    gain_one = gain_one_full.astype(jnp.float32)
    bias_one = bias_one_full.astype(jnp.float32)
    gain_two = gain_two_full.astype(jnp.float32)
    bias_two = bias_two_full.astype(jnp.float32)
    normed_one = to_half(normalize(inputs, gain_one, bias_one))
    normed_two = to_half(normalize(inputs, gain_two, bias_two))
    triple = jnp.dot(
        normed_one, triple_full, preferred_element_type=jnp.float32
    ) + triple_bias_full.astype(jnp.float32)
    cosine_table, sine_table = rotary_tables(seq_length)
    head_shape = (seq_length, head_count, HEAD_DIM)
    queries = to_half(rotate(triple[:, :model_width].reshape(head_shape), cosine_table, sine_table))
    keys = to_half(
        rotate(
            triple[:, model_width : 2 * model_width].reshape(head_shape), cosine_table, sine_table
        )
    )
    values = to_half(triple[:, 2 * model_width :].reshape(head_shape))
    block_rows = min(512, seq_length)
    score_scale = 1.0 / math.sqrt(HEAD_DIM)
    col_pos = jnp.arange(seq_length)

    def block_scores(row_start):
        scores = (
            jnp.einsum("qhe,khe->hqk", queries, keys, preferred_element_type=jnp.float32)
            * score_scale
        )
        row_pos = row_start + jnp.arange(block_rows)
        allowed = col_pos[None, :] <= row_pos[:, None]
        return (queries, jnp.where(allowed[None, :, :], scores, -1e30))

    block_index = 0
    rows_query, scores = block_scores(block_index * block_rows)
    row_max = jnp.max(scores, -1, keepdims=True)
    expon = jnp.exp(scores - row_max)
    row_total = jnp.sum(expon, -1, keepdims=True)
    probs = to_half(expon / row_total)
    log_sums = [row_max + jnp.log(row_total)]
    contexts = jnp.einsum("hqk,khe->qhe", probs, values, preferred_element_type=jnp.float32)
    context = to_half(contexts.reshape(seq_length, model_width))
    attention = jnp.dot(
        context, output_full, preferred_element_type=jnp.float32
    ) + output_bias_full.astype(jnp.float32)
    hidden = jnp.dot(
        normed_two, expand_full, preferred_element_type=jnp.float32
    ) + expand_bias_full.astype(jnp.float32)
    activated = to_half(jax.nn.gelu(hidden, approximate=False))
    feed = jnp.dot(
        activated, shrink_full, preferred_element_type=jnp.float32
    ) + shrink_bias_full.astype(jnp.float32)
    block_output = to_half(inputs + attention + feed)
    grad_out_f = output_cotangent.astype(jnp.float32)
    out_bias_grad = jnp.sum(grad_out_f, 0)
    shrink_grad = jnp.einsum(
        "tf,td->fd", activated, output_cotangent, preferred_element_type=jnp.float32
    )
    output_grad = jnp.einsum(
        "td,te->de", context, output_cotangent, preferred_element_type=jnp.float32
    )
    grad_activated = jnp.einsum(
        "td,fd->tf", output_cotangent, shrink_full, preferred_element_type=jnp.float32
    )
    _, gelu_pull = jax.vjp(lambda entries: jax.nn.gelu(entries, approximate=False), hidden)
    grad_hidden = to_half(gelu_pull(grad_activated)[0])
    expand_grad = jnp.einsum(
        "td,tf->df", normed_two, grad_hidden, preferred_element_type=jnp.float32
    )
    expand_bias_grad = jnp.sum(grad_hidden.astype(jnp.float32), 0)
    grad_normed_two = jnp.einsum(
        "tf,df->td", grad_hidden, expand_full, preferred_element_type=jnp.float32
    )
    grad_context = to_half(
        jnp.einsum("td,ed->te", output_cotangent, output_full, preferred_element_type=jnp.float32)
    ).reshape(head_shape)
    block_index = 0
    row_start = block_index * block_rows
    rows_query, scores = block_scores(row_start)
    probs = jnp.exp(scores - log_sums[block_index])
    grad_values = jnp.einsum(
        "hqk,qhe->khe", to_half(probs), grad_context, preferred_element_type=jnp.float32
    )
    grad_probs = jnp.einsum(
        "qhe,khe->hqk", grad_context, values, preferred_element_type=jnp.float32
    )
    inner_sum = jnp.sum(probs * grad_probs, -1, keepdims=True)
    grad_scores = to_half(probs * (grad_probs - inner_sum))
    grad_query_list = (
        jnp.einsum("hqk,khe->qhe", grad_scores, keys, preferred_element_type=jnp.float32)
        * score_scale
    )
    grad_keys = (
        jnp.einsum("hqk,qhe->khe", grad_scores, rows_query, preferred_element_type=jnp.float32)
        * score_scale
    )
    grad_triple = to_half(
        jnp.concatenate(
            [
                unrotate(grad_query_list, cosine_table, sine_table).reshape(
                    seq_length, model_width
                ),
                unrotate(grad_keys, cosine_table, sine_table).reshape(seq_length, model_width),
                grad_values.reshape(seq_length, model_width),
            ],
            -1,
        )
    )
    triple_grad = jnp.einsum(
        "td,te->de", normed_one, grad_triple, preferred_element_type=jnp.float32
    )
    triple_bias_grad = jnp.sum(grad_triple.astype(jnp.float32), 0)
    grad_normed_one = jnp.einsum(
        "te,de->td", grad_triple, triple_full, preferred_element_type=jnp.float32
    )
    _, norm_pull_one = jax.vjp(normalize, inputs, gain_one, bias_one)
    input_part_one, gain_one_grad, bias_one_grad = norm_pull_one(grad_normed_one)
    _, norm_pull_two = jax.vjp(normalize, inputs, gain_two, bias_two)
    input_part_two, gain_two_grad, bias_two_grad = norm_pull_two(grad_normed_two)
    input_gradient = to_half(grad_out_f + input_part_one + input_part_two)
    local_grads = (
        gain_one_grad,
        bias_one_grad,
        gain_two_grad,
        bias_two_grad,
        triple_grad,
        triple_bias_grad,
        output_grad,
        out_bias_grad,
        expand_grad,
        expand_bias_grad,
        shrink_grad,
        out_bias_grad,
    )
    owned = (
        lax.psum_scatter(local_grads[0], "shard", scatter_dimension=0, tiled=True),
        lax.psum_scatter(local_grads[1], "shard", scatter_dimension=0, tiled=True),
        lax.psum_scatter(local_grads[2], "shard", scatter_dimension=0, tiled=True),
        lax.psum_scatter(local_grads[3], "shard", scatter_dimension=0, tiled=True),
        lax.psum_scatter(local_grads[4], "shard", scatter_dimension=0, tiled=True),
        lax.psum_scatter(local_grads[5], "shard", scatter_dimension=0, tiled=True),
        lax.psum_scatter(local_grads[6], "shard", scatter_dimension=0, tiled=True),
        lax.psum_scatter(local_grads[7], "shard", scatter_dimension=0, tiled=True),
        lax.psum_scatter(local_grads[8], "shard", scatter_dimension=0, tiled=True),
        lax.psum_scatter(local_grads[9], "shard", scatter_dimension=0, tiled=True),
        lax.psum_scatter(local_grads[10], "shard", scatter_dimension=0, tiled=True),
        lax.psum_scatter(local_grads[11], "shard", scatter_dimension=0, tiled=True),
    )
    summed = lax.psum(
        (
            owned[0],
            owned[1],
            owned[2],
            owned[3],
            owned[4],
            owned[5],
            owned[6],
            owned[7],
            owned[8],
            owned[9],
            owned[10],
            owned[11],
        ),
        "grp",
    )
    updated = []
    moment_one = []
    moment_two = []
    for position_index in range(12):
        new_weight, delta, new_momentum, new_variance = adam_step(
            masters[position_index],
            summed[position_index],
            momenta[position_index],
            variances[position_index],
            position_index in (4, 6, 8, 10),
        )
        if position_index in (0, 2):
            updated.append(delta)
        else:
            updated.append(new_weight)
        moment_one.append(new_momentum)
        moment_two.append(new_variance)
    return (
        (block_output, input_gradient)
        + tuple(summed)
        + tuple(updated)
        + tuple(moment_one)
        + tuple(moment_two)
    )


def solution(mesh):
    placed = (
        P(("grp", "shard"), None),
        P(("grp", "shard"), None),
        P("shard"),
        P("shard"),
        P("shard"),
        P("shard"),
        P("shard", None),
        P("shard"),
        P("shard", None),
        P("shard"),
        P("shard", None),
        P("shard"),
        P("shard", None),
        P("shard"),
        P("shard"),
        P("shard"),
        P("shard"),
        P("shard"),
        P("shard", None),
        P("shard"),
        P("shard", None),
        P("shard"),
        P("shard", None),
        P("shard"),
        P("shard", None),
        P("shard"),
        P("shard"),
        P("shard"),
        P("shard"),
        P("shard"),
        P("shard", None),
        P("shard"),
        P("shard", None),
        P("shard"),
        P("shard", None),
        P("shard"),
        P("shard", None),
        P("shard"),
    )
    return jax.shard_map(
        on_device,
        mesh=mesh,
        in_specs=placed,
        out_specs=(
            P(("grp", "shard"), None),
            P(("grp", "shard"), None),
            P("shard"),
            P("shard"),
            P("shard"),
            P("shard"),
            P("shard", None),
            P("shard"),
            P("shard", None),
            P("shard"),
            P("shard", None),
            P("shard"),
            P("shard", None),
            P("shard"),
            P("shard"),
            P("shard"),
            P("shard"),
            P("shard"),
            P("shard", None),
            P("shard"),
            P("shard", None),
            P("shard"),
            P("shard", None),
            P("shard"),
            P("shard", None),
            P("shard"),
            P("shard"),
            P("shard"),
            P("shard"),
            P("shard"),
            P("shard", None),
            P("shard"),
            P("shard", None),
            P("shard"),
            P("shard", None),
            P("shard"),
            P("shard", None),
            P("shard"),
            P("shard"),
            P("shard"),
            P("shard"),
            P("shard"),
            P("shard", None),
            P("shard"),
            P("shard", None),
            P("shard"),
            P("shard", None),
            P("shard"),
            P("shard", None),
            P("shard"),
        ),
        check_vma=False,
    )
```

profile of v0, /device:TPU:27, one launch (start us, length us, event | category | flops | bytes accessed | tf_op | source)
XLA Modules:
  0.0 1556.1 jit_solution(18349632124645426292)
XLA Ops:
  19.6 11.7 all-gather.2
  31.4 8.6 all-gather.1
  40.0 8.4 all-gather
  49.9 74.8 %all-gather.12.cloned.1.call-done = bf16[1024,3072]{1,0:T(8,128)(2,1)} async-done(((bf16[256,3072]{1,0:T(8,128)(2,1)}), bf16[1024,3072]{1,0:T(8,128)(2,1)}) %all-gather.12.cloned.1.call-update) | async-done | bytes 6291472 | tf_op jit(solution)/shard_map/all_gather | solution.py:173
  149.2 8.7 fusion.79
  158.0 8.4 fusion
  166.4 7.6 fusion.38
  183.7 17.8 %multiply_reduce_fusion = (f32[16,512]{1,0:T(8,128)}, f32[16,512,512]{1,2,0:T(8,128)}) fusion(f32[16,512,512]{1,2,0:T(8,128)} %get-tuple-element.145, f32[16,512]{1,0:T(8,128)} %log_add_fusion, bf16[512,16,64]{0,2,1:T(8,128)(2,1)} %bitcast.50, bf16[512,16,64]{0,2,1:T(8,128)(2,1)} %bitcast.59), kind=kOutput, calls=%fused_computation.1 | convolution fusion | flops 549445632 | bytes 35717120 | tf_op jit(solution)/shard_map/qhe,khe->hqk/dot_general | solution.py:280
  201.6 8.1 multiply_convert_fusion
  227.3 10.3 fusion.59
  238.3 15.4 all-gather.5
  259.6 17.4 %all_gather.45 = bf16[4096]{0:T(1024)(128)(2,1)S(1)} all-gather(bf16[1024]{0:T(1024)(128)(2,1)S(1)} %convert_element_type.217), channel_id=1, replica_groups=mesh['grp'=8,'shard'=4] {'shard'}, dimensions={0}, use_global_device_ids=true | all-gather | bytes 10240 | tf_op jit(solution)/shard_map/all_gather | solution.py:178
  277.0 44.5 %all-gather.16.cloned.1.call-done = bf16[1024,4096]{1,0:T(8,128)(2,1)} async-done(((bf16[256,4096]{1,0:T(8,128)(2,1)}), bf16[1024,4096]{1,0:T(8,128)(2,1)}) %all-gather.16.cloned.1.call-update) | async-done | bytes 8388624 | tf_op jit(solution)/shard_map/all_gather | solution.py:177
  321.6 10.4 fusion.57
  332.0 139.4 %all-gather.18.cloned.1.call-done = bf16[4096,1024]{1,0:T(8,128)(2,1)} async-done(((bf16[1024,1024]{1,0:T(8,128)(2,1)}), bf16[4096,1024]{1,0:T(8,128)(2,1)}) %all-gather.18.cloned.1.call-update) | async-done | bytes 8388624 | tf_op jit(solution)/shard_map/all_gather | solution.py:179
  471.4 27.3 %convert_reduce_fusion = (f32[4096]{0:T(1024)S(1)}, bf16[512,4096]{1,0:T(8,128)(2,1)S(1)}, f32[512,4096]{1,0:T(8,128)}) fusion(f32[512,4096]{1,0:T(8,128)} %fusion.57, f32[4096]{0:T(1024)S(1)} %convert_element_type.218, bf16[512,1024]{1,0:T(8,128)(2,1)S(1)} %copy-done.23, bf16[4096,1024]{1,0:T(8,128)(2,1)} %all-gather.18.cloned.1.call-done), kind=kOutput, calls=%fused_computation.11 | convolution fusion | flops 4452249600 | bytes 30441472 | tf_op jit(solution)/shard_map/td,fd->tf/dot_general | solution.py:258
  500.7 8.5 fusion.55
  509.5 7.8 multiply_convert_fusion.1
  519.4 8.2 fusion.83
  532.9 8.3 fusion.81
  541.2 10.0 reduce-scatter.7.cloned.1.call-done
  551.2 215.2 %reduce-scatter.5.cloned.1.call-done = f32[256,3072]{1,0:T(8,128)} async-done(((f32[1024,3072]{1,0:T(8,128)}), f32[256,3072]{1,0:T(8,128)}) %reduce-scatter.5.cloned.1.call-update) | async-done | bytes 3145744 | tf_op jit(solution)/shard_map/reduce_scatter | solution.py:336
  766.4 283.5 %reduce-scatter.9.cloned.1.call-done = f32[256,4096]{1,0:T(8,128)} async-done(((f32[1024,4096]{1,0:T(8,128)}), f32[256,4096]{1,0:T(8,128)}) %reduce-scatter.9.cloned.1.call-update) | async-done | bytes 4194320 | tf_op jit(solution)/shard_map/reduce_scatter | solution.py:340
  1049.9 283.5 %reduce-scatter.11.cloned.1.call-done = f32[1024,1024]{1,0:T(8,128)} async-done(((f32[4096,1024]{1,0:T(8,128)}), f32[1024,1024]{1,0:T(8,128)}) %reduce-scatter.11.cloned.1.call-update) | async-done | bytes 4194320 | tf_op jit(solution)/shard_map/reduce_scatter | solution.py:342
  1333.3 7.7 fusion.66
  1345.7 12.7 all-reduce.9
  1358.9 26.1 %all-reduce.7 = (f32[256]{0:T(256)S(1)}, f32[256]{0:T(256)S(1)}, f32[256]{0:T(256)S(1)}, f32[256]{0:T(256)S(1)}, f32[768]{0:T(1024)S(1)}, /*index=5*/f32[256]{0:T(256)S(1)}, f32[1024]{0:T(1024)S(1)}) all-reduce(f32[256]{0:T(256)S(1)} %dynamic-slice.1, f32[256]{0:T(256)S(1)} %dynamic-slice.3, ...), channel_id=1, replica_groups=mesh['grp'=8,'shard'=4] {'grp'}, use_global_device_ids=true, to_apply=%region_11.12 | all-reduce | flops 3072 | bytes 24576 | tf_op jit(solution)/shard_map/psum | solution.py:345
  1385.8 8.6 all-gather.6
  1403.6 9.3 fusion.80
  1415.3 95.4 %all-reduce.12.cloned.1.call-done = (f32[256,3072]{1,0:T(8,128)}, f32[256,1024]{1,0:T(8,128)}, f32[256,4096]{1,0:T(8,128)}, f32[1024,1024]{1,0:T(8,128)}) async-done(((f32[256,3072]{1,0:T(8,128)}, f32[256,1024]{1,0:T(8,128)}, f32[256,4096]{1,0:T(8,128)}, f32[1024,1024]{1,0:T(8,128)}), (f32[256,3072]{1,0:T(8,128)}, f32[256,1024]{1,0:T(8,128)}, f32[256,4096]{1,0:T(8,128)}, ...) | async-done | bytes 12582928 | tf_op jit(solution)/shard_map/psum | solution.py:345
  1510.8 8.4 multiply_add_fusion.4
  1533.3 8.6 multiply_add_fusion
  (264 shorter events, 118.2 us)
Async XLA Ops:
  7.3 117.5 %all-gather.12.cloned.1.call-start = ((), (), s32[]{:S(2)}) async-start(), calls=%async_computation.4 | async-start | bytes 7864320 | tf_op jit(solution)/shard_map/all_gather | solution.py:173
  10.7 168.2 %all-gather.14.cloned.1.call-start = ((), (), s32[]{:S(2)}) async-start(), calls=%async_computation.5 | async-start | bytes 2621440 | tf_op jit(solution)/shard_map/all_gather | solution.py:175
  11.6 310.0 %all-gather.16.cloned.1.call-start = ((), (), s32[]{:S(2)}) async-start(), calls=%async_computation.6 | async-start | bytes 10485760 | tf_op jit(solution)/shard_map/all_gather | solution.py:177
  15.5 455.9 %all-gather.18.cloned.1.call-start = ((), (), s32[]{:S(2)}) async-start(), calls=%async_computation.7 | async-start | bytes 10485760 | tf_op jit(solution)/shard_map/all_gather | solution.py:179
  19.5 531.7 %reduce-scatter.7.cloned.1.call-start = ((), (), s32[]{:S(2)}) async-start(), calls=%async_computation.9 | async-start | bytes 5242880 | tf_op jit(solution)/shard_map/reduce_scatter | solution.py:338
  40.0 90.5 %copy-start.47 = (f32[4,1,256]{2,1,0:T(1,128)}, f32[4,1,256]{2,1,0:T(1,128)S(1)}, u32[]{:S(2)}) copy-start(f32[4,1,256]{2,1,0:T(1,128)S(1)} %convert_element_type.233) | copy-start | bytes 12292
  49.9 97.6 %copy-start.31 = (f32[512,8]{0,1:T(8,128)}, f32[512,8]{0,1:T(8,128)S(1)}, u32[]{:S(2)}) copy-start(f32[512,8]{0,1:T(8,128)S(1)} %get-tuple-element.135) | copy-start | bytes 49156
  49.9 97.6 %copy-start.33 = (f32[512,8]{0,1:T(8,128)}, f32[512,8]{0,1:T(8,128)S(1)}, u32[]{:S(2)}) copy-start(f32[512,8]{0,1:T(8,128)S(1)} %get-tuple-element.136) | copy-start | bytes 49156
  178.3 588.1 %reduce-scatter.5.cloned.1.call-start = ((), (), s32[]{:S(2)}) async-start(), calls=%async_computation.8 | async-start | bytes 15728640 | tf_op jit(solution)/shard_map/reduce_scatter | solution.py:336
  237.6 812.2 %reduce-scatter.9.cloned.1.call-start = ((), (), s32[]{:S(2)}) async-start(), calls=%async_computation.10 | async-start | bytes 20971520 | tf_op jit(solution)/shard_map/reduce_scatter | solution.py:340
  321.6 149.8 %copy-start.23 = (bf16[512,1024]{1,0:T(8,128)(2,1)S(1)}, bf16[512,1024]{1,0:T(8,128)(2,1)}, u32[]{:S(2)}) copy-start(bf16[512,1024]{1,0:T(8,128)(2,1)} %param.39) | copy-start | bytes 3145732
  509.3 824.0 %reduce-scatter.11.cloned.1.call-start = ((), (), s32[]{:S(2)}) async-start(), calls=%async_computation.11 | async-start | bytes 20971520 | tf_op jit(solution)/shard_map/reduce_scatter | solution.py:342
  527.7 983.0 %all-reduce.12.cloned.1.call-start = ((), (), s32[]{:S(2)}) async-start(), calls=%async_computation.12 | async-start | bytes 25165824 | tf_op jit(solution)/shard_map/psum | solution.py:345
  1343.0 42.1 %copy-start.48 = (f32[256]{0:T(256)S(1)}, f32[256]{0:T(256)}, u32[]{:S(2)}) copy-start(f32[256]{0:T(256)} %param.51) | copy-start | bytes 3076
  1343.0 42.1 %copy-start.49 = (f32[256]{0:T(256)S(1)}, f32[256]{0:T(256)}, u32[]{:S(2)}) copy-start(f32[256]{0:T(256)} %param.63) | copy-start | bytes 3076
  1343.0 42.1 %copy-start.50 = (f32[256]{0:T(256)S(1)}, f32[256]{0:T(256)}, u32[]{:S(2)}) copy-start(f32[256]{0:T(256)} %param.75) | copy-start | bytes 3076
  1343.0 42.1 %copy-start.51 = (f32[256]{0:T(256)S(1)}, f32[256]{0:T(256)}, u32[]{:S(2)}) copy-start(f32[256]{0:T(256)} %param.47) | copy-start | bytes 3076
  1343.1 56.9 %copy-start.63 = (f32[256]{0:T(256)S(1)}, f32[256]{0:T(256)}, u32[]{:S(2)}) copy-start(f32[256]{0:T(256)} %param.52) | copy-start | bytes 3076
  1343.1 56.9 %copy-start.64 = (f32[256]{0:T(256)S(1)}, f32[256]{0:T(256)}, u32[]{:S(2)}) copy-start(f32[256]{0:T(256)} %param.64) | copy-start | bytes 3076
  1343.1 57.5 %copy-start.65 = (f32[256]{0:T(256)S(1)}, f32[256]{0:T(256)}, u32[]{:S(2)}) copy-start(f32[256]{0:T(256)} %param.54) | copy-start | bytes 3076
  1343.1 57.5 %copy-start.66 = (f32[256]{0:T(256)S(1)}, f32[256]{0:T(256)}, u32[]{:S(2)}) copy-start(f32[256]{0:T(256)} %param.66) | copy-start | bytes 3076
  1343.1 58.0 %copy-start.55 = (f32[256]{0:T(256)S(1)}, f32[256]{0:T(256)}, u32[]{:S(2)}) copy-start(f32[256]{0:T(256)} %param.41) | copy-start | bytes 3076
  1343.1 58.0 %copy-start.56 = (f32[256]{0:T(256)S(1)}, f32[256]{0:T(256)}, u32[]{:S(2)}) copy-start(f32[256]{0:T(256)} %param.53) | copy-start | bytes 3076
  1343.1 58.0 %copy-start.57 = (f32[256]{0:T(256)S(1)}, f32[256]{0:T(256)}, u32[]{:S(2)}) copy-start(f32[256]{0:T(256)} %param.65) | copy-start | bytes 3076
  1343.1 58.6 %copy-start.59 = (f32[256]{0:T(256)S(1)}, f32[256]{0:T(256)}, u32[]{:S(2)}) copy-start(f32[256]{0:T(256)} %param.55) | copy-start | bytes 3076
  1343.2 58.6 %copy-start.60 = (f32[256]{0:T(256)S(1)}, f32[256]{0:T(256)}, u32[]{:S(2)}) copy-start(f32[256]{0:T(256)} %param.67) | copy-start | bytes 3076
  1343.2 59.2 %copy-start.38 = (f32[768]{0:T(1024)S(1)}, f32[768]{0:T(1024)}, u32[]{:S(2)}) copy-start(f32[768]{0:T(1024)} %param.45) | copy-start | bytes 9220
  1343.2 59.2 %copy-start.41 = (f32[768]{0:T(1024)S(1)}, f32[768]{0:T(1024)}, u32[]{:S(2)}) copy-start(f32[768]{0:T(1024)} %param.57) | copy-start | bytes 9220
  1343.2 59.1 %copy-start.42 = (f32[768]{0:T(1024)S(1)}, f32[768]{0:T(1024)}, u32[]{:S(2)}) copy-start(f32[768]{0:T(1024)} %param.69) | copy-start | bytes 9220
  1343.2 59.8 %copy-start.43 = (f32[1024]{0:T(1024)S(1)}, f32[1024]{0:T(1024)}, u32[]{:S(2)}) copy-start(f32[1024]{0:T(1024)} %param.61) | copy-start | bytes 12292
  1343.2 59.7 %copy-start.44 = (f32[1024]{0:T(1024)S(1)}, f32[1024]{0:T(1024)}, u32[]{:S(2)}) copy-start(f32[1024]{0:T(1024)} %param.73) | copy-start | bytes 12292
  1385.1 156.8 %copy-start.40 = (f32[256]{0:T(256)}, f32[256]{0:T(256)S(1)}, u32[]{:S(2)}) copy-start(f32[256]{0:T(256)S(1)} %get-tuple-element.260) | copy-start | bytes 3076
  (57 other events, 698.3 us)
Sparse Core Ops, SparseCore 0:
  10.8 113.8 all-gather.11
  126.8 44.4 all-gather.13
  173.5 148.0 all-gather.15
  323.6 147.7 all-gather.17
  474.1 77.0 reduce-scatter.6
  553.4 212.8 reduce-scatter.4
  768.7 281.0 reduce-scatter.8
  1052.2 281.0 reduce-scatter.10
  1337.3 173.3 all-reduce.11
where the time goes:
time: 1570 us; the launch traced here: 1560 us
  waiting for transfers between devices  1150 us (73%)
  matrix products  151 us (10%)
  blocking collectives  120 us (8%)
  other arithmetic  77.8 us (5%)
  local copies, waits for them, and re-layouts  41.7 us (3%)
  between operations  17.3 us (1%)
    reduce_scatter x1, waiting for transfers between devices, on_device(): lax.psum_scatter(local_grads[8], 'shard', scatter_dimension=0, tiled=True)  283 us
    reduce_scatter x1, waiting for transfers between devices, on_device(): lax.psum_scatter(local_grads[10], 'shard', scatter_dimension=0, tiled=True)  283 us
    reduce_scatter x1, waiting for transfers between devices, on_device(): lax.psum_scatter(local_grads[4], 'shard', scatter_dimension=0, tiled=True)  215 us
    all_gather x1, waiting for transfers between devices, on_device(): lax.all_gather(to_half(shrink_weight), 'shard', axis=0, tiled=True)  139 us
    psum x1, waiting for transfers between devices, on_device(): lax.psum((owned[0], owned[1], owned[2], owned[3], owned[4], owned[5], own...  95.4 us
    all_gather x1, waiting for transfers between devices, on_device(): lax.all_gather(to_half(triple_weight), 'shard', axis=0, tiled=True)  74.8 us
    all_gather x1, waiting for transfers between devices, on_device(): lax.all_gather(to_half(expand_weight), 'shard', axis=0, tiled=True)  44.5 us
  transfers between devices with their start and end apart: 9, of which 8 were waited for; matrix products, arithmetic and copies ran while one was open for 14% of the time, Pallas kernels for 0%

commit v1 on v0

v1 whole, which is shorter than its diff:
```python
import math

import jax
import jax.numpy as jnp
from jax import lax
from jax.experimental import pallas as pl
from jax.experimental.pallas import tpu as pltpu
from jax.sharding import Mesh, PartitionSpec as P

HEAD_DIM = 64
ROTARY = 16
STEP = 10
eps_norm = 1e-05
rope_base = 10000.0
beta_one = 0.9
beta_two = 0.95
learn_rate = 0.01
adam_eps = 1e-08
weight_decay = 0.01

bf16 = jnp.bfloat16
f32 = jnp.float32


def adam_step(weight, gradient, momentum, variance, decayed):
    momentum_new = beta_one * momentum + (1.0 - beta_one) * gradient
    variance_new = beta_two * variance + (1.0 - beta_two) * gradient * gradient
    mean_hat = momentum_new / (1.0 - beta_one**STEP)
    var_hat = variance_new / (1.0 - beta_two**STEP)
    change = mean_hat / (jnp.sqrt(var_hat) + adam_eps)
    if decayed:
        change = change + weight_decay * weight
    delta = -learn_rate * change
    return (weight + delta, delta, momentum_new, variance_new)


def rotary_tables(length):
    position = jnp.arange(length).astype(f32)[:, None]
    half = ROTARY // 2
    inverse_freq = rope_base ** (-(jnp.arange(half).astype(f32) * 2.0 / ROTARY))
    angles = position * inverse_freq[None, :]
    return jnp.cos(angles), jnp.sin(angles)


def rotate(tensor, cosine, sine):
    half = ROTARY // 2
    a, b, rest = tensor[..., :half], tensor[..., half:ROTARY], tensor[..., ROTARY:]
    return jnp.concatenate([a * cosine - b * sine, b * cosine + a * sine, rest], -1)


def dot32(a, b, dims):
    return lax.dot_general(a, b, (dims, ((), ())), preferred_element_type=f32)


MESH = pl.DeviceIdType.MESH
ANY = pl.BlockSpec(memory_space=pl.ANY)
VM = pl.BlockSpec(memory_space=pltpu.VMEM)
ONE = ((1,), (0,))
NT = ((1,), (1,))
TN = ((0,), (0,))


def rows_of(start, size):
    return pl.ds(pl.multiple_of(start, math.gcd(size, 512)), size)


class Links:
    def __init__(self, R, X, S):
        self.R, self.X, self.S = R, X, S
        self.rep = lax.axis_index("rep")
        self.tx = lax.axis_index("tx")
        self.core = lax.axis_index("core")
        self.z = lax.axis_index("shard")

    def at_core(self):
        return {"core": 1 - self.core}

    def at_tx(self):
        return {"tx": 1 - self.tx}

    def at_rep(self, dr):
        return {"rep": lax.rem(self.rep + dr, self.R)}

    def at_z(self, z):
        return {"shard": z}

    def barrier(self):
        sem = pltpu.get_barrier_semaphore()

        def tell(where):
            pl.semaphore_signal(sem, inc=1, device_id=where, device_id_type=MESH)

        count = 1 + (self.X - 1) + (self.R - 1)
        tell(self.at_core())
        if self.X > 1:
            tell(self.at_tx())
        for dr in range(1, self.R):
            tell(self.at_rep(dr))

        @pl.when(self.z > 0)
        def _():
            tell(self.at_z(self.z - 1))

        @pl.when(self.z < self.S - 1)
        def _():
            tell(self.at_z(self.z + 1))

        ends = (self.z > 0).astype(jnp.int32) + (self.z < self.S - 1).astype(jnp.int32)
        pl.semaphore_wait(sem, count + ends)


def remote(src, dst, send, recv, where):
    return pltpu.make_async_remote_copy(
        src_ref=src, dst_ref=dst, send_sem=send, recv_sem=recv, device_id=where, device_id_type=MESH
    )


def local(src, dst, sem):
    return pltpu.make_async_copy(src, dst, sem)


class LineGather:
    def __init__(self, links, own, buf, n, zs, zr, ys, yr, split):
        self.k = links
        self.own, self.buf, self.n = own, buf, n
        self.parts = links.R if split else 1
        self.m = n // self.parts
        self.zs, self.zr, self.ys, self.yr = zs, zr, ys, yr

    def block(self, p, r):
        return self.buf.at[rows_of(p * self.n + r * self.m, self.m)]

    def mine(self):
        return self.k.rep if self.parts > 1 else 0

    def hop(self, src, p, step, way):
        to = self.k.z + 1 if way == 0 else self.k.z - 1
        return remote(
            src, self.block(p, self.mine()), self.zs.at[step, way], self.zr.at[p], self.k.at_z(to)
        )

    def across(self, p, dr):
        b = self.block(p, self.k.rep)
        return remote(b, b, self.ys.at[p, dr], self.yr.at[p, self.k.rep], self.k.at_rep(dr))

    def each_way(self, step, fn):
        z, S = self.k.z, self.k.S
        for way in (0, 1):
            p = z - step if way == 0 else z + step
            here = (step <= z) if way == 0 else (z + step <= S - 1)
            on = (z < S - 1) if way == 0 else (z > 0)
            fn(way, p, here, on)

    def start(self):
        mine = self.mine()

        def go(way, p, here, on):
            @pl.when(on)
            def _():
                self.hop(self.own.at[rows_of(mine * self.m, self.m)], p, 0, way).start()

        self.each_way(0, go)

    def event(self, step):
        def go(way, p, here, on):
            @pl.when(here)
            def _():
                b = self.block(p, self.mine())
                self.hop(b, p, step, way).wait_recv()

                @pl.when(on)
                def _():
                    self.hop(b, p, step, way).start()

                if self.parts > 1:
                    for dr in range(1, self.k.R):
                        self.across(p, dr).start()

        self.each_way(step, go)

    def arrived(self):
        if self.parts == 1:
            return
        for p in range(self.k.S):
            @pl.when(p != self.k.z)
            def _():
                for dr in range(1, self.k.R):
                    r = lax.rem(self.k.rep + dr, self.k.R)
                    b = self.block(p, r)
                    remote(b, b, self.ys.at[p, dr], self.yr.at[p, r], self.k.at_rep(dr)).wait_recv()

    def drain(self):
        for step in range(self.k.S):
            def go(way, p, here, on):
                @pl.when(jnp.logical_and(here, on))
                def _():
                    self.hop(self.block(p, self.mine()), p, step, way).wait_send()

                if step > 0 and self.parts > 1:
                    @pl.when(here)
                    def _():
                        for dr in range(1, self.k.R):
                            self.across(p, dr).wait_send()

            self.each_way(step, go)


def layer_norm_rows(xb):
    xf = xb.astype(f32)
    cen = xf - jnp.mean(xf, -1, keepdims=True)
    return cen * lax.rsqrt(jnp.mean(cen * cen, -1, keepdims=True) + eps_norm)


SMALL_ROWS = 24


def small_row(sm, S, first, count):
    return jnp.concatenate(
        [sm[p * SMALL_ROWS + first + j : p * SMALL_ROWS + first + j + 1, :] for p in range(S) for j in range(count)],
        -1,
    )


def attention_kernel(R, X, S, L, D, FT, *refs):
    (x_ref, dy_ref, wt_ref, wo_ref, we_ref, ws_ref, sm_ref, rc_ref, ra_ref, rb_ref) = refs[:10]
    (xg, dyg, wt_o, wo_o, we_o, ws_o, vec_o, ctx_o, gt_o, wtg_o, wog_o, tbg_o) = refs[10:22]
    (
        xs, dys, n1, gt, wtb, wob, smb, q_s, k_s, v_s, gc_s, kT, vT, ctxT, gqT, gk_a, gv_a, wtg, wog,
        zs, zr, ys, yr, tok_s, tok_r, loc,
    ) = refs[22:]
    T = 2 * X
    rows = D // S
    DT = S * HEAD_DIM
    links = Links(R, X, S)
    chunks = []
    for c, (own, buf) in enumerate(
        [(sm_ref, smb), (wt_ref, wtb), (wo_ref, wob), (we_ref, we_o), (ws_ref, ws_o)]
    ):
        chunks.append(
            LineGather(links, own, buf, own.shape[0], zs.at[c], zr.at[c], ys.at[c], yr.at[c], c > 0)
        )
    g_sm, g_wt, g_wo, g_we, g_ws = chunks
    links.barrier()

    own_copies = [
        local(x_ref, xs.at[pl.ds(0, L)], loc.at[0]),
        local(dy_ref, dys.at[pl.ds(0, L)], loc.at[1]),
    ]
    for c, g in enumerate(chunks):
        own_copies.append(local(g.own, g.buf.at[rows_of(links.z * g.n, g.n)], loc.at[2 + c]))

    def token_copy(a, slot):
        buf = (xs, dys)[a]
        src = (x_ref, dy_ref)[a]
        if slot == 1:
            return remote(src, buf.at[pl.ds(L, L)], tok_s.at[a, 1], tok_r.at[a, 1], links.at_core())
        if slot == 2:
            return remote(src, buf.at[pl.ds(2 * L, L)], tok_s.at[a, 2], tok_r.at[a, 2], links.at_tx())
        return remote(
            buf.at[pl.ds(2 * L, L)], buf.at[pl.ds(3 * L, L)], tok_s.at[a, 3], tok_r.at[a, 3], links.at_core()
        )

    g_sm.start()
    g_wt.start()
    g_wo.start()
    if X > 1:
        token_copy(0, 2).start()
        token_copy(1, 2).start()
    token_copy(0, 1).start()
    token_copy(1, 1).start()
    for c in own_copies:
        c.start()

    own_copies[0].wait()
    own_copies[2].wait()
    for step in range(1, S):
        g_sm.event(step)
    per = rows // 128
    vec_o[...] = jnp.zeros_like(vec_o)
    sm = smb[...]
    for j in range(6):
        vec_o[j : j + 1, 0:D] = small_row(sm, S, j * per, per)
    fper = FT // S // 128
    vec_o[8 : 8 + 1, 0:FT] = small_row(sm, S, 6 * per, fper)
    lane = lax.broadcasted_iota(jnp.int32, (1, 128), 1)
    rank = links.tx * 2 + links.core

    def head_bias(j, p):
        block = j * (D // 128) + (T * p + rank) // 2
        at = (block // (3 * per)) * SMALL_ROWS + 6 * per + fper + lax.rem(block, 3 * per)
        row = smb[pl.ds(at, 1), :]
        return jnp.where(lax.rem(rank, 2) == p % 2, row, pltpu.roll(row, HEAD_DIM, 1))

    for j in range(3):
        for a in range(S // 2):
            both = jnp.where(lane < HEAD_DIM, head_bias(j, 2 * a), head_bias(j, 2 * a + 1))
            vec_o[9 + j : 10 + j, a * 128 : (a + 1) * 128] = both

    def norm_one(i):
        gain, shift = vec_o[0:1, 0:D], vec_o[1:2, 0:D]

        @pl.loop(0, L // 64)
        def _(b):
            at = rows_of(i * L + b * 64, 64)
            n1[at, :] = (layer_norm_rows(xs[at, :]) * gain + shift).astype(bf16)

    norm_one(0)
    g_wt.event(1)
    g_wo.event(1)
    g_we.start()
    for step in range(2, S):
        g_wt.event(step)
        g_wo.event(step)
    g_ws.start()
    own_copies[1].wait()
    own_copies[3].wait()
    own_copies[4].wait()
    g_wt.arrived()
    g_wo.arrived()
    late = [(g, step) for step in range(1, S) for g in (g_we, g_ws)]

    def pump(i, turn):
        for index in range(T):
            at = 2 * (2 * index + turn)
            todo = late[at : at + 2]
            if todo:
                @pl.when(i == index)
                def _():
                    for g, step in todo:
                        g.event(step)

    half = L // 2
    lane_head = lax.broadcasted_iota(jnp.int32, (1, DT), 1) // HEAD_DIM
    key_at = lax.broadcasted_iota(jnp.int32, (half, half), 0)
    query_at = lax.broadcasted_iota(jnp.int32, (half, half), 1)
    causal = key_at <= query_at

    def slot_body(i, carry):
        here = rows_of(i * L, L)
        for j, dst in enumerate((q_s, k_s, v_s)):
            val = dot32(n1[here, :], wtb[:, j * DT : (j + 1) * DT], ONE) + vec_o[9 + j : 10 + j, 0:DT]
            if j < 2:
                val = (
                    val * rc_ref[...]
                    + pltpu.roll(val, DT - 8, 1) * ra_ref[...]
                    + pltpu.roll(val, 8, 1) * rb_ref[...]
                )
            vb = val.astype(bf16)
            if j == 0:
                q_s[...] = vb * bf16(0.125)
            else:
                dst[...] = vb
                (kT if j == 1 else vT)[...] = vb.T
        gc_s[...] = dot32(dys[here, :], wob[...], NT).astype(bf16)
        gk_a[...] = jnp.zeros_like(gk_a)
        gv_a[...] = jnp.zeros_like(gv_a)
        pump(i, 0)

        def head_body(h, c2):
            mine = (lane_head == h).astype(f32).astype(bf16)
            hrows = rows_of(h * HEAD_DIM, HEAD_DIM)
            for b in range(2):
                qs = pl.ds(b * half, half)
                kl = (b + 1) * half
                km = k_s[0:kl, :] * mine
                sT = dot32(km, q_s[qs, :], NT)
                diag = jnp.where(causal, sT[kl - half :], -1e30)
                sT = diag if b == 0 else jnp.concatenate([sT[: kl - half], diag], 0)
                e = jnp.exp(sT - jnp.max(sT, 0, keepdims=True))
                p = e * (1.0 / jnp.sum(e, 0, keepdims=True))
                pb = p.astype(bf16)
                ctxT[hrows, qs] = dot32(vT[hrows, 0:kl], pb, ONE).astype(bf16)
                gv_a[0:kl, :] += dot32(pb, gc_s[qs, :] * mine, ONE)
                gp = dot32(v_s[0:kl, :] * mine, gc_s[qs, :], NT)
                gs = (p * (gp - jnp.sum(p * gp, 0, keepdims=True))).astype(bf16)
                gk_a[0:kl, :] += dot32(gs, q_s[qs, :] * mine, ONE)
                gqT[hrows, qs] = dot32(kT[hrows, 0:kl], gs, ONE) * 0.125
            return c2

        lax.fori_loop(0, S, head_body, 0)
        pump(i, 1)
        for j in range(3):
            if j == 2:
                val = gv_a[...]
            else:
                val = gqT[...].T if j == 0 else gk_a[...]
                val = (
                    val * rc_ref[...]
                    - pltpu.roll(val, DT - 8, 1) * ra_ref[...]
                    - pltpu.roll(val, 8, 1) * rb_ref[...]
                )
            gt[here, j * DT : (j + 1) * DT] = val.astype(bf16)
        ctx_o[:, rows_of(i * L, L)] = ctxT[...]
        grad = dot32(ctxT[...], dys[here, :], ONE)

        @pl.when(i == 0)
        def _():
            wog[...] = grad

        @pl.when(i > 0)
        def _():
            wog[...] += grad

        if X > 1:
            @pl.when(i == 1)
            def _():
                for a in (0, 1):
                    token_copy(a, 2).wait_recv()
                    token_copy(a, 3).start()

        for nxt in range(1, T):
            @pl.when(i + 1 == nxt)
            def _():
                for a in (0, 1):
                    if nxt != 2:
                        token_copy(a, nxt).wait_recv()

        @pl.when(i + 1 < T)
        def _():
            norm_one(i + 1)

        return carry

    lax.fori_loop(0, T, slot_body, 0)
    outs = [
        local(xs, xg, loc.at[0]),
        local(dys, dyg, loc.at[1]),
        local(wtb, wt_o, loc.at[3]),
        local(wob, wo_o, loc.at[4]),
        local(gt, gt_o, loc.at[7]),
        local(wog, wog_o, loc.at[8]),
    ]
    for o in outs:
        o.start()
    for g, step in late[4 * T :]:
        g.event(step)
    ones = jnp.ones((8, T * L), bf16)
    tbg_o[...] = dot32(ones, gt[...], ONE)

    @pl.loop(0, D // 256)
    def _(b):
        at = rows_of(b * 256, 256)
        wtg[at, :] = dot32(n1[:, pl.ds(pl.multiple_of(b * 256, 256), 256)], gt[...], TN)

    last = local(wtg, wtg_o, loc.at[9])
    last.start()
    own_copies[5].wait()
    own_copies[6].wait()
    g_we.arrived()
    g_ws.arrived()
    for g in chunks:
        g.drain()
    for a in (0, 1):
        for slot in range(1, T):
            token_copy(a, slot).wait_send()
    for o in outs:
        o.wait()
    last.wait()


def attention_phase(R, X, S, x, dy, wt, wo, we, ws, small, tables):
    L, D = x.shape
    T = 2 * X
    DT = S * HEAD_DIM
    FT = we.shape[1]
    fs = ws.shape[0]
    n = T * L
    sds = jax.ShapeDtypeStruct
    dma = pltpu.SemaphoreType.DMA
    outs = [
        sds((n, D), bf16), sds((n, D), bf16), sds((D, 3 * DT), bf16), sds((DT, D), bf16),
        sds((D, FT), bf16), sds((FT, D), bf16), sds((16, max(D, FT)), f32), sds((DT, n), bf16),
        sds((n, 3 * DT), bf16), sds((D, 3 * DT), f32), sds((DT, D), f32), sds((8, 3 * DT), f32),
    ]
    specs = [ANY] * 6 + [VM, VM] + [ANY] * 3 + [VM]
    vmem = pltpu.VMEM
    scratch = [
        vmem((n, D), bf16), vmem((n, D), bf16), vmem((n, D), bf16), vmem((n, 3 * DT), bf16),
        vmem((D, 3 * DT), bf16), vmem((DT, D), bf16), vmem((S * SMALL_ROWS, 128), f32),
        vmem((L, DT), bf16), vmem((L, DT), bf16), vmem((L, DT), bf16), vmem((L, DT), bf16),
        vmem((DT, L), bf16), vmem((DT, L), bf16), vmem((DT, L), bf16), vmem((DT, L), f32),
        vmem((L, DT), f32), vmem((L, DT), f32), vmem((D, 3 * DT), f32), vmem((DT, D), f32),
        dma((5, S, 2)), dma((5, S)), dma((5, S, R)), dma((5, S, R)), dma((2, 4)), dma((2, 4)), dma((10,)),
    ]
    body = lambda *refs: attention_kernel(R, X, S, L, D, FT, *refs)
    return pl.pallas_call(
        body,
        name="attention_phase",
        out_shape=outs,
        in_specs=[ANY] * 7 + [VM] * 3,
        out_specs=specs,
        scratch_shapes=scratch,
        compiler_params=pltpu.CompilerParams(
            collective_id=1, has_side_effects=True, vmem_limit_bytes=60 * 1024 * 1024
        ),
    )(x, dy, wt, wo, we, ws, small, *tables)


TP = ("tx", "core")


def make_step(R, X, S):
    T = 2 * X

    def step(*args):
        x, dy = args[0], args[1]
        masters, momenta, variances = args[2:14], args[14:26], args[26:38]
        L, D = x.shape
        H = D // HEAD_DIM
        t = lax.axis_index(TP)
        z = lax.axis_index("shard")
        rep = lax.axis_index("rep")
        wt, wo, we, ws = masters[4], masters[6], masters[8], masters[10]
        rows = wt.shape[0]
        F = we.shape[1]
        fs = F // S // T
        HT = H // T

        low = [lax.reduce_precision(m, 8, 7) for m in masters]
        eb_own = lax.dynamic_index_in_dim(low[9].reshape(T, fs), t, 0, False)
        packed = [low[i].reshape(-1, 128) for i in (0, 1, 2, 3, 7, 11)] + [eb_own.reshape(-1, 128)]
        packed.append(low[5].reshape(-1, 128))
        packed = jnp.concatenate(packed)
        small = jnp.pad(packed, ((0, SMALL_ROWS - packed.shape[0]), (0, 0)))

        wt_t = lax.dynamic_index_in_dim(wt.reshape(rows, 3, S, T, HEAD_DIM), t, 3, False)
        wt_t = wt_t.reshape(rows, 3 * S * HEAD_DIM).astype(bf16)
        we_t = lax.dynamic_index_in_dim(we.reshape(rows, S, T, fs), t, 2, False)
        we_t = we_t.reshape(rows, S * fs).astype(bf16)
        wo_t = lax.dynamic_index_in_dim(wo.reshape(T, rows // T, D), t, 0, False).astype(bf16)
        ws_t = lax.dynamic_index_in_dim(ws.reshape(T, fs, D), t, 0, False).astype(bf16)

        cosine, sine = rotary_tables(L)
        zero, one = jnp.zeros((L, 8), f32), jnp.ones((L, HEAD_DIM - 16), f32)
        pad = jnp.zeros((L, HEAD_DIM - 16), f32)
        tables = (
            jnp.tile(jnp.concatenate([cosine, cosine, one], 1), (1, S)),
            jnp.tile(jnp.concatenate([-sine, zero, pad], 1), (1, S)),
            jnp.tile(jnp.concatenate([zero, sine, pad], 1), (1, S)),
        )
        (xg, dyg, wt_f, wo_f, we_f, ws_f, vecs, ctxT, gt, wt_g, wo_g, tb_g) = attention_phase(
            R, X, S, x, dy, wt_t, wo_t, we_t, ws_t, small, tables
        )
        g1v, b1v, g2v, b2v, obv, sbv = [vecs[i, :D] for i in range(6)]
        eb_t = vecs[8, :F // T]
        tb_g = tb_g[0]
        xf = xg.astype(f32)
        cen = xf - jnp.mean(xf, -1, keepdims=True)
        rstd = lax.rsqrt(jnp.mean(cen * cen, -1, keepdims=True) + eps_norm)
        xhat = cen * rstd
        n2 = (xhat * g2v + b2v).astype(bf16)
        hidden = dot32(n2, we_f, ((1,), (0,))) + eb_t
        act32, gelu_pull = jax.vjp(lambda e: jax.nn.gelu(e, approximate=False), hidden)
        act = act32.astype(bf16)
        out_part = dot32(ctxT, wo_f, TN) + dot32(act, ws_f, ((1,), (0,)))

        def scatter_tokens(part):
            part = part.astype(bf16)
            slots = part.reshape(T, L, D)
            order = jnp.bitwise_xor(jnp.arange(T), t)
            part = jnp.take(slots, order, axis=0).reshape(X, 2, L, D)
            part = lax.psum_scatter(part, "core", scatter_dimension=1, tiled=False)
            part = lax.psum_scatter(part, "tx", scatter_dimension=0, tiled=False)
            return part.astype(f32)

        xl = x.astype(f32)
        out = (xl + scatter_tokens(out_part) + (obv + sbv)).astype(bf16)

        dact = dot32(dyg, ws_f, ((1,), (1,)))
        gh = gelu_pull(dact)[0].astype(bf16)
        ws_g = dot32(act, dyg, ((0,), (0,)))
        we_g = dot32(n2, gh, ((0,), (0,)))
        gn2 = dot32(gh, we_f, ((1,), (1,)))
        eb_g = jnp.sum(gh.astype(f32), 0)
        gn1 = dot32(gt, wt_f, ((1,), (1,)))

        dxhat = scatter_tokens(gn1 * g1v + gn2 * g2v)
        cl = xl - jnp.mean(xl, -1, keepdims=True)
        rl = lax.rsqrt(jnp.mean(cl * cl, -1, keepdims=True) + eps_norm)
        xh = cl * rl
        dx = rl * (
            dxhat
            - jnp.mean(dxhat, -1, keepdims=True)
            - xh * jnp.mean(dxhat * xh, -1, keepdims=True)
        )
        in_grad = (dy.astype(f32) + dx).astype(bf16)

        vec = jnp.concatenate(
            [
                jnp.sum(gn1 * xhat, 0),
                jnp.sum(gn1, 0),
                jnp.sum(gn2 * xhat, 0),
                jnp.sum(gn2, 0),
                jnp.sum(dy.astype(f32), 0),
                jnp.where(
                    jnp.arange(T)[None, None, :, None] == t,
                    tb_g.reshape(3, S, 1, HEAD_DIM),
                    0.0,
                ).reshape(-1),
                jnp.where(
                    jnp.arange(T)[None, :, None] == t, eb_g.reshape(S, 1, fs), 0.0
                ).reshape(-1),
            ]
        )
        vec = lax.psum(vec, ("rep", "tx", "core", "shard"))
        vparts = [D] * 5 + [3 * D, F]
        voffs = [sum(vparts[:i]) for i in range(8)]
        vown = [
            lax.dynamic_slice_in_dim(vec, voffs[i] + z * (vparts[i] // S), vparts[i] // S, 0)
            for i in range(7)
        ]

        def reduce_w(grad):
            n = grad.shape[0] // S
            grad = grad.reshape(S, R, n // R, grad.shape[1])
            grad = lax.psum_scatter(grad, "rep", scatter_dimension=1, tiled=False)
            grad = lax.psum_scatter(grad, "shard", scatter_dimension=0, tiled=False)
            grad = lax.all_gather(grad.astype(bf16), "rep", axis=0, tiled=True)
            return lax.all_gather(grad, TP, axis=0).astype(f32)

        wt_s = reduce_w(wt_g).reshape(T, rows, 3, S, HEAD_DIM).transpose(1, 2, 3, 0, 4)
        wt_s = wt_s.reshape(rows, 3 * D)
        wo_s = reduce_w(wo_g).reshape(rows, D)
        we_s = reduce_w(we_g).reshape(T, rows, S, fs).transpose(1, 2, 0, 3).reshape(rows, F)
        ws_s = reduce_w(ws_g).reshape(F // S, D)

        summed = [
            vown[0], vown[1], vown[2], vown[3], wt_s, vown[5], wo_s, vown[4], we_s, vown[6], ws_s, vown[4],
        ]
        updated, ones, twos = [], [], []
        for i in range(12):
            new_weight, delta, m_new, v_new = adam_step(
                masters[i], summed[i], momenta[i], variances[i], i in (4, 6, 8, 10)
            )
            updated.append(delta if i in (0, 2) else new_weight)
            ones.append(m_new)
            twos.append(v_new)
        return (out, in_grad, *summed, *updated, *ones, *twos)

    return step


def solution(mesh):
    G, S = mesh.shape["grp"], mesh.shape["shard"]
    X = 2 if S <= 4 else 1
    R = G // (2 * X)
    full = Mesh(mesh.devices.reshape(R, X, 2, S), ("rep", "tx", "core", "shard"))
    tok = P(("rep", "tx", "core", "shard"), None)
    vecs, mats = P("shard"), P("shard", None)
    group = tuple(mats if i in (4, 6, 8, 10) else vecs for i in range(12))
    return jax.shard_map(
        make_step(R, X, S),
        mesh=full,
        in_specs=(tok, tok) + group * 3,
        out_specs=(tok, tok) + group * 4,
        check_vma=False,
    )
```

time: 1570 us -> 805 us (0.51)
  waiting for transfers between devices: 1150 us -> 360 us
  Pallas kernels: 0 us -> 93.8 us
  matrix products: 151 us -> 80.4 us
  local copies, waits for them, and re-layouts: 41.7 us -> 93.2 us
  blocking collectives: 120 us -> 78.6 us
    reduce_scatter x4 -> x7, waiting for transfers between devices: 792 us -> 153 us  [the longest x4 115 us: reduce_w(): grad = lax.psum_scatter(grad, 'shard', scatter_dimension=0, tiled=False)]
    all_gather x4 -> x3, waiting for transfers between devices: 259 us -> 0.22 us  [reduce_w(): return lax.all_gather(grad, TP, axis=0).astype(f32)]
    unnamed x9 -> x14, waiting for transfers between devices: 0.15 us -> 206 us
    psum x1 -> x0, waiting for transfers between devices: 95.4 us -> none  [on_device(): lax.psum((owned[0], owned[1], owned[2], owned[3], owned[4], owned[5], own...]
    pallas_call x0 -> x1, Pallas kernels: none -> 93.8 us  [attention_phase(): pl.pallas_call(body, name='attention_phase', out_shape=outs, in_specs=[AN...]
    dot_general x18 -> x8, matrix products: 151 us -> 80.4 us  [dot32(): return lax.dot_general(a, b, (dims, ((), ())), preferred_element_type=f32)]
    all_gather x8 -> x5, blocking collectives: 81.6 us -> 37.7 us  [the longest x4 25.9 us: reduce_w(): grad = lax.all_gather(grad.astype(bf16), 'rep', axis=0, tiled=True)]
    reshape x0 -> x7, local copies, waits for them, and re-layouts: none -> 26.3 us  [the longest x3 17.6 us: step(): reduce_w(we_g).reshape(T, rows, S, fs).transpose(1, 2, 0, 3)]
  transfers between devices with their start and end apart: 9 -> 12, of which waited for: 8 -> 9; matrix products, arithmetic and copies ran while one was open for 14% -> 26% of each run, Pallas kernels for 0% -> 0%
where the time goes in v1:
time: 805 us; the launch traced here: 793 us
  waiting for transfers between devices  360 us (45%)
  Pallas kernels  93.8 us (12%)
  local copies, waits for them, and re-layouts  93.2 us (12%)
  matrix products  80.4 us (10%)
  blocking collectives  78.6 us (10%)
  other arithmetic  70.9 us (9%)
  between operations  15.6 us (2%)
    unnamed x14, waiting for transfers between devices  206 us
    reduce_scatter x4, waiting for transfers between devices, reduce_w(): grad = lax.psum_scatter(grad, 'shard', scatter_dimension=0, tiled=False)  115 us
    pallas_call x1, Pallas kernels, attention_phase(): pl.pallas_call(body, name='attention_phase', out_shape=outs, in_specs=[AN...  93.8 us
    dot_general x8, matrix products, dot32(): return lax.dot_general(a, b, (dims, ((), ())), preferred_element_type=f32)  80.4 us
    psum x1, blocking collectives, step(): vec = lax.psum(vec, ('rep', 'tx', 'core', 'shard'))  40.9 us
    reduce_scatter x2, waiting for transfers between devices, scatter_tokens(): part = lax.psum_scatter(part, 'tx', scatter_dimension=0, tiled=False)  38.4 us
    add x8, other arithmetic, adam_step(): return (weight + delta, delta, momentum_new, variance_new)  34.3 us
    all_gather x4, blocking collectives, reduce_w(): grad = lax.all_gather(grad.astype(bf16), 'rep', axis=0, tiled=True)  25.9 us
  transfers between devices with their start and end apart: 12, of which 9 were waited for; matrix products, arithmetic and copies ran while one was open for 26% of the time, Pallas kernels for 0%

profile of v1, /device:TPU:27, one launch (start us, length us, event | category | flops | bytes accessed | tf_op | source)
XLA Modules:
  0.0 793.2 jit_solution(11325551558251305485)
XLA Ops:
  12.5 4.5 reshape.296
  27.5 93.8 %attention_phase.1 = (bf16[2048,1024]{1,0:T(8,128)(2,1)}, bf16[2048,1024]{1,0:T(8,128)(2,1)}, bf16[1024,768]{1,0:T(8,128)(2,1)}, bf16[256,1024]{1,0:T(8,128)(2,1...) custom-call(bf16[512,1024]{1,0:T(8,128)(2,1)} %refs_0_.1, ...), custom_call_target="tpu_custom_call" | custom-call | tf_op jit(solution)/shard_map/attention_phase/pallas_call | solution.py:486
  131.9 5.2 fusion.45
  137.1 25.4 %convert_reduce_fusion.1 = (f32[1024]{0:T(1024)S(1)}, bf16[2048,1024]{1,0:T(8,128)(2,1)}, f32[2048,1024]{1,0:T(8,128)}) fusion(f32[2048,1024]{1,0:T(8,128)S(1)} %fusion.45, f32[1024]{0:T(1024)S(1)} %bitcast.157, bf16[2048,1024]{1,0:T(8,128)(2,1)S(1)} %copy-done.45, bf16[1024,1024]{1,0:T(8,128)(2,1)S(1)} %copy-done.46), kind=kOutput, calls=%fused_computation.16 | convolution fusion | flops 4452252672 | bytes 27271168 | tf_op jit(solution)/shard_map/dot_general | solution.py:52
  162.5 10.1 %multiply_convert_fusion = bf16[2048,1024]{1,0:T(8,128)(2,1)} fusion(f32[2048,1024]{1,0:T(8,128)} %get-tuple-element.281, f32[2048,1024]{1,0:T(8,128)} %copy-done.6, f32[1024]{0:T(1024)S(1)} %bitcast.158), kind=kLoop, calls=%fused_computation.20 | loop fusion | flops 8388608 | bytes 20975616 | tf_op jit(solution)/shard_map/convert_element_type | solution.py:554
  172.6 10.2 %fusion.62 = f32[1024,1024]{1,0:T(8,128)} fusion(bf16[2048,1024]{1,0:T(8,128)(2,1)} %multiply_convert_fusion, bf16[2048,1024]{1,0:T(8,128)(2,1)} %get-tuple-element.71), kind=kOutput, calls=%fused_computation.166 | convolution fusion | flops 4294967296 | bytes 12582912 | tf_op jit(solution)/shard_map/dot_general | solution.py:52
  182.8 7.3 fusion.43
  190.4 9.6 %fusion.61 = f32[2048,1024]{1,0:T(8,128)} fusion(bf16[2048,768]{1,0:T(8,128)(2,1)} %get-tuple-element.69, bf16[1024,768]{1,0:T(8,128)(2,1)} %get-tuple-element.70), kind=kOutput, calls=%fused_computation.165 | convolution fusion | flops 3221225472 | bytes 13107200 | tf_op jit(solution)/shard_map/dot_general | solution.py:52
  200.1 12.8 %fusion.47 = (f32[1024]{0:T(1024)S(1)}, f32[1024]{0:T(1024)S(1)}, bf16[2048,1024]{1,0:T(8,128)(2,1)}, f32[1024]{0:T(1024)S(1)}, f32[1024]{0:T(1024)S(1)}) fusion(f32[2048]{0:T(1024)S(1)} %add_rsqrt_fusion, f32[2048]{0:T(1024)S(1)} %broadcast_multiply_fusion, bf16[2048,1024]{1,0:T(8,128)(2,1)} %get-tuple-element.65, f32[1024]{0:T(1024)S(1)} %bitcast.163, ...), kind=kOutput, calls=%fused_computation.162 | convolution fusion | flops 4322226176 | bytes 23109632 | tf_op jit(solution)/shard_map/dot_general | solution.py:52
  212.9 5.0 gather_fusion.1
  218.0 6.5 fusion.60
  227.8 5.0 gather_fusion
  232.9 8.0 %broadcast_select_fusion = (bf16[4,512,1024]{2,1,0:T(8,128)(2,1)}, bf16[4,512,1024]{2,1,0:T(8,128)(2,1)}) fusion(bf16[4,512,1024]{2,1,0:T(8,128)(2,1)} %gather_fusion.1, pred[4]{0:T(512)(128)(4,1)S(1)} %get-tuple-element.316, bf16[4,512,1024]{2,1,0:T(8,128)(2,1)} %gather_fusion), kind=kLoop, calls=%fused_computation.43 | loop fusion | flops 4194304 | bytes 16777220 | tf_op jit(solution)/shard_map/jit(_take)/select_n | solution.py:561
  242.1 171.1 %all-reduce.11.cloned.1.call-done = (f32[4,2,128,1024]{3,2,1,0:T(8,128)}, f32[4,2,32,1024]{3,2,1,0:T(8,128)}, f32[4,2,128,1024]{3,2,1,0:T(8,128)}) async-done(((f32[4,2,128,1024]{3,2,1,0:T(8,128)}, f32[4,2,32,1024]{3,2,1,0:T(8,128)}, f32[4,2,128,1024]{3,2,1,0:T(8,128)}), (f32[4,2,128,1024]{3,2,1,0:T(8,128)}, f32[4,2,32,1024]{3,2,1,0:T(8,128)}, f32[4,2,128,1024]{3,2,1,0:T(8,128)})) %all-reduce.11.cloned.1.call-update) | async-done | bytes 9437200
  419.7 29.3 %reduce-scatter.29.cloned.1.call-done = f32[1,128,768]{2,1,0:T(8,128)} async-done(((f32[4,128,768]{2,1,0:T(8,128)}), f32[1,128,768]{2,1,0:T(8,128)}) %reduce-scatter.29.cloned.1.call-update) | async-done | bytes 393232 | tf_op jit(solution)/shard_map/reduce_scatter | solution.py:617
  450.0 6.4 all-gather
  457.1 35.0 %all-reduce.13.cloned.1.call-done = (bf16[2,2,512,1024]{3,2,1,0:T(8,128)(2,1)}, bf16[2,2,512,1024]{3,2,1,0:T(8,128)(2,1)}) async-done(((bf16[2,2,512,1024]{3,2,1,0:T(8,128)(2,1)}, bf16[2,2,512,1024]{3,2,1,0:T(8,128)(2,1)}), (bf16[2,2,512,1024]{3,2,1,0:T(8,128)(2,1)}, bf16[2,2,512,1024]{3,2,1,0:T(8,128)(2,1)})) %all-reduce.13.cloned.1.call-update) | async-done | bytes 8388624
  499.9 4.0 dynamic-slice_bitcast_fusion.3
  517.9 42.1 %reduce-scatter.33.cloned.1.call-done = f32[1,128,1024]{2,1,0:T(8,128)} async-done(((f32[4,128,1024]{2,1,0:T(8,128)}), f32[1,128,1024]{2,1,0:T(8,128)}) %reduce-scatter.33.cloned.1.call-update) | async-done | bytes 524304 | tf_op jit(solution)/shard_map/reduce_scatter | solution.py:617
  561.0 7.8 all-gather.4
  568.9 11.8 %all-gather.3 = bf16[4,64,1024]{2,1,0:T(8,128)(2,1)S(1)} all-gather(bf16[1,64,1024]{2,1,0:T(8,128)(2,1)S(1)} %all-gather.2), channel_id=5, replica_groups=mesh['rep'=2,'tx'=2,'core'=2,'shard'=4] {'tx','core'}, dimensions={0}, use_global_device_ids=true | all-gather | bytes 655360 | tf_op jit(solution)/shard_map/all_gather | solution.py:619
  589.4 6.9 multiply_add_fusion.4
  606.0 12.8 %reduce-scatter.25.cloned.1.call-done = bf16[1,512,1024]{2,1,0:T(8,128)(2,1)} async-done(((bf16[2,512,1024]{2,1,0:T(8,128)(2,1)}), bf16[1,512,1024]{2,1,0:T(8,128)(2,1)}) %reduce-scatter.25.cloned.1.call-update) | async-done | bytes 1048592 | tf_op jit(solution)/shard_map/reduce_scatter | solution.py:563
  622.3 42.1 %reduce-scatter.35.cloned.1.call-done = f32[1,128,1024]{2,1,0:T(8,128)} async-done(((f32[4,128,1024]{2,1,0:T(8,128)}), f32[1,128,1024]{2,1,0:T(8,128)}) %reduce-scatter.35.cloned.1.call-update) | async-done | bytes 524304 | tf_op jit(solution)/shard_map/reduce_scatter | solution.py:617
  665.5 7.8 all-gather.6
  673.4 25.7 %reduce-scatter.23.cloned.1.call-done = bf16[1,512,1024]{2,1,0:T(8,128)(2,1)} async-done(((bf16[2,512,1024]{2,1,0:T(8,128)(2,1)}), bf16[1,512,1024]{2,1,0:T(8,128)(2,1)}) %reduce-scatter.23.cloned.1.call-update) | async-done | bytes 1048592 | tf_op jit(solution)/shard_map/reduce_scatter | solution.py:563
  702.7 40.9 %psum.7 = f32[12288]{0:T(1024)S(1)} all-reduce(f32[12288]{0:T(1024)S(1)} %constant_dynamic-update-slice_fusion), channel_id=1, replica_groups=mesh['rep'=2,'tx'=2,'core'=2,'shard'=4] {'rep','tx','core','shard'}, use_global_device_ids=true, to_apply=%region_16.18 | all-reduce | flops 12288 | bytes 98304 | tf_op jit(solution)/shard_map/psum | solution.py:605
  746.5 5.0 reshape.339
  751.5 6.9 copy.137
  758.4 5.8 reshape.331
  764.2 11.1 %multiply_add_fusion.2 = (f32[256,4096]{1,0:T(8,128)}, f32[256,4096]{1,0:T(8,128)}, f32[256,4096]{1,0:T(8,128)}) fusion(f32[256,4096]{1,0:T(8,128)} %param.50, f32[256,4096]{1,0:T(8,128)} %reshape.331, f32[256,4096]{1,0:T(8,128)} %param.62, f32[256,4096]{1,0:T(8,128)} %param.74), kind=kLoop, calls=%fused_computation.41 | loop fusion | flops 15728640 | bytes 29360128 | tf_op jit(solution)/shard_map/add | solution.py:34
  775.3 10.1 %multiply_add_fusion = (f32[1024,1024]{1,0:T(8,128)}, f32[1024,1024]{1,0:T(8,128)}, f32[1024,1024]{1,0:T(8,128)}, f32[1024,1024]{1,0:T(8,128)}) fusion(f32[1024,1024]{1,0:T(8,128)} %param.52, f32[1024,1024]{1,0:T(8,128)} %param.64, f32[1024,1024]{1,0:T(8,128)} %param.76, bf16[4,256,1024]{2,1,0:T(8,128)(2,1)} %all-gather.16.cloned.1.call-done), kind=kLoop, calls=%fused_computation.39 | loop fusion | flops 16777216 | bytes 31457280 | tf_op jit(solution)/shard_map/add | solution.py:34
  (222 shorter events, 91.4 us)
Async XLA Ops:
  7.2 192.8 %reduce-scatter.27.cloned.1.call-start = ((), (), s32[]{:S(2)}) async-start(), calls=%async_computation.9 | async-start | bytes 4718592 | tf_op jit(solution)/shard_map/reduce_scatter | solution.py:616
  125.2 288.1 %all-reduce.11.cloned.1.call-start = ((), (), s32[]{:S(2)}) async-start(), calls=%async_computation.17 | async-start | bytes 18874368
  190.2 258.8 %reduce-scatter.29.cloned.1.call-start = ((), (), s32[]{:S(2)}) async-start(), calls=%async_computation.10 | async-start | bytes 1966080 | tf_op jit(solution)/shard_map/reduce_scatter | solution.py:617
  200.0 292.1 %all-reduce.13.cloned.1.call-start = ((), (), s32[]{:S(2)}) async-start(), calls=%async_computation.18 | async-start | bytes 16777216
  240.9 272.3 %reduce-scatter.31.cloned.1.call-start = ((), (), s32[]{:S(2)}) async-start(), calls=%async_computation.11 | async-start | bytes 655360 | tf_op jit(solution)/shard_map/reduce_scatter | solution.py:617
  415.8 144.2 %reduce-scatter.33.cloned.1.call-start = ((), (), s32[]{:S(2)}) async-start(), calls=%async_computation.12 | async-start | bytes 2621440 | tf_op jit(solution)/shard_map/reduce_scatter | solution.py:617
  419.7 164.9 %all-gather.12.cloned.1.call-start = ((), (), s32[]{:S(2)}) async-start(), calls=%async_computation.14 | async-start | bytes 1966080 | tf_op jit(solution)/shard_map/all_gather | solution.py:619
  456.5 162.2 %reduce-scatter.25.cloned.1.call-start = ((), (), s32[]{:S(2)}) async-start(), calls=%async_computation.8 | async-start | bytes 3145728 | tf_op jit(solution)/shard_map/reduce_scatter | solution.py:563
  495.9 168.5 %reduce-scatter.35.cloned.1.call-start = ((), (), s32[]{:S(2)}) async-start(), calls=%async_computation.13 | async-start | bytes 2621440 | tf_op jit(solution)/shard_map/reduce_scatter | solution.py:617
  499.8 199.3 %reduce-scatter.23.cloned.1.call-start = ((), (), s32[]{:S(2)}) async-start(), calls=%async_computation.7 | async-start | bytes 3145728 | tf_op jit(solution)/shard_map/reduce_scatter | solution.py:563
  503.9 242.6 %all-gather.14.cloned.1.call-start = ((), (), s32[]{:S(2)}) async-start(), calls=%async_computation.15 | async-start | bytes 2621440 | tf_op jit(solution)/shard_map/all_gather | solution.py:619
  568.9 206.4 %all-gather.16.cloned.1.call-start = ((), (), s32[]{:S(2)}) async-start(), calls=%async_computation.16 | async-start | bytes 2621440 | tf_op jit(solution)/shard_map/all_gather | solution.py:619
  622.1 121.6 %copy-start.26 = (f32[256]{0:T(256)S(1)}, f32[256]{0:T(256)}, u32[]{:S(2)}) copy-start(f32[256]{0:T(256)} %param.43) | copy-start | bytes 3076
  622.1 121.5 %copy-start.28 = (f32[256]{0:T(256)S(1)}, f32[256]{0:T(256)}, u32[]{:S(2)}) copy-start(f32[256]{0:T(256)} %param.45) | copy-start | bytes 3076
  622.1 121.5 %copy-start.30 = (f32[256]{0:T(256)S(1)}, f32[256]{0:T(256)}, u32[]{:S(2)}) copy-start(f32[256]{0:T(256)} %param.53) | copy-start | bytes 3076
  622.1 121.5 %copy-start.35 = (f32[256]{0:T(256)S(1)}, f32[256]{0:T(256)}, u32[]{:S(2)}) copy-start(f32[256]{0:T(256)} %param.65) | copy-start | bytes 3076
  622.1 121.5 %copy-start.36 = (f32[256]{0:T(256)S(1)}, f32[256]{0:T(256)}, u32[]{:S(2)}) copy-start(f32[256]{0:T(256)} %param.77) | copy-start | bytes 3076
  622.1 121.5 %copy-start.37 = (f32[256]{0:T(256)S(1)}, f32[256]{0:T(256)}, u32[]{:S(2)}) copy-start(f32[256]{0:T(256)} %param.69) | copy-start | bytes 3076
  622.1 121.5 %copy-start.38 = (f32[256]{0:T(256)S(1)}, f32[256]{0:T(256)}, u32[]{:S(2)}) copy-start(f32[256]{0:T(256)} %param.57) | copy-start | bytes 3076
  622.2 121.5 %copy-start.39 = (f32[256]{0:T(256)S(1)}, f32[256]{0:T(256)}, u32[]{:S(2)}) copy-start(f32[256]{0:T(256)} %param.68) | copy-start | bytes 3076
  622.2 121.5 %copy-start.40 = (f32[256]{0:T(256)S(1)}, f32[256]{0:T(256)}, u32[]{:S(2)}) copy-start(f32[256]{0:T(256)} %param.56) | copy-start | bytes 3076
  622.2 121.5 %copy-start.41 = (f32[256]{0:T(256)S(1)}, f32[256]{0:T(256)}, u32[]{:S(2)}) copy-start(f32[256]{0:T(256)} %param.67) | copy-start | bytes 3076
  622.2 121.5 %copy-start.42 = (f32[256]{0:T(256)S(1)}, f32[256]{0:T(256)}, u32[]{:S(2)}) copy-start(f32[256]{0:T(256)} %param.55) | copy-start | bytes 3076
  622.2 122.3 %copy-start.20 = (f32[256]{0:T(256)S(1)}, f32[256]{0:T(256)}, u32[]{:S(2)}) copy-start(f32[256]{0:T(256)} %param.49) | copy-start | bytes 3076
  622.2 122.3 %copy-start.31 = (f32[256]{0:T(256)S(1)}, f32[256]{0:T(256)}, u32[]{:S(2)}) copy-start(f32[256]{0:T(256)} %param.61) | copy-start | bytes 3076
  622.2 122.3 %copy-start.32 = (f32[256]{0:T(256)S(1)}, f32[256]{0:T(256)}, u32[]{:S(2)}) copy-start(f32[256]{0:T(256)} %param.73) | copy-start | bytes 3076
  622.3 122.9 %copy-start.15 = (f32[768]{0:T(1024)S(1)}, f32[768]{0:T(1024)}, u32[]{:S(2)}) copy-start(f32[768]{0:T(1024)} %param.47) | copy-start | bytes 9220
  622.3 122.9 %copy-start.21 = (f32[768]{0:T(1024)S(1)}, f32[768]{0:T(1024)}, u32[]{:S(2)}) copy-start(f32[768]{0:T(1024)} %param.59) | copy-start | bytes 9220
  622.3 122.9 %copy-start.22 = (f32[768]{0:T(1024)S(1)}, f32[768]{0:T(1024)}, u32[]{:S(2)}) copy-start(f32[768]{0:T(1024)} %param.71) | copy-start | bytes 9220
  622.3 123.6 %copy-start.17 = (f32[1024]{0:T(1024)S(1)}, f32[1024]{0:T(1024)}, u32[]{:S(2)}) copy-start(f32[1024]{0:T(1024)} %param.51) | copy-start | bytes 12292
  622.3 123.6 %copy-start.23 = (f32[1024]{0:T(1024)S(1)}, f32[1024]{0:T(1024)}, u32[]{:S(2)}) copy-start(f32[1024]{0:T(1024)} %param.63) | copy-start | bytes 12292
  622.3 123.6 %copy-start.24 = (f32[1024]{0:T(1024)S(1)}, f32[1024]{0:T(1024)}, u32[]{:S(2)}) copy-start(f32[1024]{0:T(1024)} %param.75) | copy-start | bytes 12292
  (31 other events, 889.8 us)
Sparse Core Ops, SparseCore 0:
  125.3 45.6 reduce-scatter.26
  190.3 222.8 all-reduce.10
  415.5 33.4 reduce-scatter.28
  452.5 39.5 all-reduce.12
  494.9 18.2 reduce-scatter.30
  515.9 43.9 reduce-scatter.32
  561.5 22.9 all-gather.11
  587.3 31.3 reduce-scatter.24
  621.6 42.8 reduce-scatter.34
  667.1 31.9 reduce-scatter.22
  700.6 23.4 all-gather.13
  725.6 23.1 all-gather.15
